TPU v7x, 32 devices: a whole 2x2x4 slice. The times are simulated.
32 devices in a mesh: task: 2 (over core), row: 16 (over z, y, x).
Axes of the slice: x: 2, y: 2, z: 4, core: 2. Of those that a mesh axis runs over, the one named last changes fastest.
Arguments:
- activation_grams: float32 [2, 7168, 7168], P('task', 'row'), may hold values from -240 to 240, as said below
- adjusted_weights: bfloat16 [2, 7168, 2048], P('task', 'row'), may hold values from -0.59765625 to 0.59765625
Outputs:
- reduced_gram: float32 [7168, 7168], P('row')
- reduced_rhs: float32 [7168, 2048], P('row')
Inputs may be any that keep to these rules, and one draw needn't show every extreme that they name: Each activation_grams[m] is symmetric and positive definite.
All inputs are finite; a program needn't handle non-finite values.
Results may differ from a plain program's by a relative error of at most 0.0003.
Values may be sent and summed in bfloat16 or wider, within the bound.
A program may use at most 192 MiB of HBM per device.

v0:
```python
import functools

import jax
import jax.numpy as jnp
from jax import lax
from jax.experimental import pallas as pl
from jax.experimental.pallas import tpu as pltpu
from jax.sharding import PartitionSpec as P

PANEL_STEPS = 2
MESH = pl.DeviceIdType.MESH
HIGHEST = lax.Precision.HIGHEST
NN = (((1,), (0,)), ((), ()))
NT = (((1,), (1,)), ((), ()))
TN = (((0,), (0,)), ((), ()))

TWO = (
    (100000, 110000, 120000, 200010, 210010, 220011, 230010, 300020, 310020, 320020, 330021, 400030, 410030, 430030),
    (100001, 110001, 120001, 200011, 210011, 220010, 230011, 300021, 310021, 320021, 330020, 400031, 410031, 430031),
    (100010, 110010, 121000, 200110, 210021, 220000, 230021, 300120, 310011, 320011, 330030, 400020, 410020, 431030),
    (100101, 111000, 121001, 200111, 210000, 220001, 230020, 300121, 310030, 320010, 330031, 400131, 411030, 431031),
    (100021, 110021, 120101, 200030, 210020, 221010, 230030, 300000, 310010, 320000, 331020, 400011, 410011, 430131),
    (100020, 111010, 121101, 200031, 210031, 221111, 230031, 300001, 310001, 320001, 331121, 400010, 411020, 431131),
    (100030, 110011, 121021, 200100, 211020, 220100, 230120, 300130, 311010, 320110, 330130, 400000, 410021, 431011),
    (100031, 110031, 211031, 231011, 311001, 321021, 400001, 410001),
    (100120, 111021, 211030, 231111, 311000, 321121, 400110, 411011),
    (100131, 111030, 230130, 320100, 400101, 411000),
)

ONE = (
    (100000, 110000, 120000, 200010, 210010, 220010, 230010, 300020, 310020, 320020, 330020, 400030, 410030, 430030),
    (100010, 110010, 200000, 210000, 220000, 230020, 300030, 310030, 320010, 330030, 400020, 410020),
    (100020, 110020, 200110, 211000, 220110, 230030, 300120, 311030, 320000, 330120, 400010, 410010),
    (100030, 111020, 121020, 200030, 210030, 221100, 231100, 300000, 310000, 321130, 331130, 400000, 411010, 431010),
    (100110, 111030, 221110, 230130, 320100, 331120, 400120, 411000),
)
FIRST = (
    (100001, 110001, 120000, 200010, 210010, 220011, 230010, 300021, 310020, 320021, 330020, 400031, 410030, 430031),
    (100101, 110000, 120001, 200000, 210000, 220000, 230020, 300020, 310011, 320011, 331021, 400130, 411031, 430130),
    (100100, 110020, 121101, 200100, 210001, 220001, 231000, 300000, 310000, 320000, 330130, 400011, 410021, 431131),
    (100120, 110010, 121001, 200011, 211021, 220101, 231010, 300001, 311000, 320001, 331131, 400000, 410000, 431031),
    (100020, 111010, 121120, 200130, 211011, 220010, 231021, 300101, 310031, 321100, 330031, 400001, 410001, 430030),
    (101021, 111021, 121110, 201121, 211130, 220110, 231130, 300030, 311021, 320010, 330030, 400101, 411011, 431011),
    (101130, 111130, 120120, 201131, 210011, 221110, 231011, 300130, 311020, 321020, 331031, 400010, 410010, 431111),
    (101011, 111011, 200020, 221010, 231031, 320131, 330021, 400021, 411020, 430121),
    (101031, 111031, 230121, 320111, 401020, 411010),
    (101030, 110011, 230131, 321030, 400121, 410020),
)
SIDE, LINE, LANE, PAD = 2, 4, 128, 512


def decoded(table):
    rounds = []
    for codes in table:
        acts = []
        for code in codes:
            z, link, a, b, s, part = (int(c) for c in str(code))
            acts.append((z - 1, link, (a, b, s, part)))
        rounds.append(acts)
    return rounds


def landed(act):
    z, link, (a, b, s, part) = act
    if link == 0:
        return z, (1 - a, b, s, part)
    if link == 1:
        return z, (a, 1 - b, s, part)
    return (z + 1 if link == 2 else z - 1), (a, b, s, part)


def pair_order(rounds):
    orders, ready = [], []
    for z in range(LINE):
        last = {(b, s): -1 for b in range(SIDE) for s in range(LINE)}
        for k, acts in enumerate(rounds):
            for act in acts:
                to, (_, b, s, _) = landed(act)
                if to == z:
                    last[b, s] = k
        ranked = sorted(last, key=lambda pair: (last[pair], pair))
        orders.append(ranked)
        ready.append([last[pair] for pair in ranked])
    return orders, [max(r[i] for r in ready) for i in range(SIDE * LINE)]


def mm(left, right, dims=NN):
    return lax.dot_general(left, right, dims, precision=HIGHEST, preferred_element_type=jnp.float32)


def bf(left, right, dims=NN):
    return lax.dot_general(left, right, dims, preferred_element_type=jnp.float32)


def halves(value):
    high = value.astype(jnp.bfloat16)
    return high, (value - high.astype(jnp.float32)).astype(jnp.bfloat16)


def iota(shape, dim):
    return lax.broadcasted_iota(jnp.int32, shape, dim)


def kernel(
    g, w, em, eo, fm, fo, wg, xg,
    gpa, gpv, gt, wv, trown, trs, sv, xs, xrv, xrp, xpk, zacc, zsend, zrecv, rsb, rt, cw, li, xpm, xpo, xp2, dref, bref, cref, uref,
    ahl, xh, xl, rhl, wt,
    wsend, wrecv, xsend, xrecv, rsend, rrecv, asend, arecv, local, tsem, dsend, drecv, esend, erecv, elocal, fsend, frecv, flocal, wsem,
):
    f32 = jnp.float32
    rows, width = g.shape
    columns = w.shape[1]
    nodes = trs.shape[0]
    half, pair = rows // 2, 2 * rows
    packed = xpk.shape[0]
    part_rows = packed // 2
    blocks = columns // LANE
    me = lax.axis_index("row")
    t = lax.axis_index("task")
    x, y, z = me % 2, (me // 2) % 2, me // 4
    two, one, early = decoded(TWO), decoded(ONE), decoded(FIRST)
    last_one = len(one) - 1
    links = ((t, me + 1 - 2 * x), (t, me + 2 - 4 * y), (t, me + 4), (t, me - 4))
    partner = (1 - t, me)

    def node_of(chunk):
        a, b, s, _ = chunk
        return s * 4 + (y + b - 2 * b * y) * 2 + (x + a - 2 * a * x)

    def by_z(fn):
        for value in range(LINE):
            @pl.when(z == value)
            def _():
                fn(value)

    def remote(src, dst, send, recv, target):
        return pltpu.make_async_remote_copy(
            src_ref=src, dst_ref=dst, send_sem=send, recv_sem=recv, device_id=target, device_id_type=MESH
        )

    def w_slot(chunk):
        start = node_of(chunk) * rows + chunk[3] * half
        return wg.at[pl.ds(pl.multiple_of(start, half), half)]

    def x_slot(chunk):
        start = node_of(chunk) * packed + chunk[3] * part_rows
        return xg.at[pl.ds(pl.multiple_of(start, 8), part_rows)]

    def a_slot(chunk):
        return rt.at[node_of(chunk)]

    def w_own(part):
        return w.at[pl.ds(part * half, half)]

    def x_own(part):
        return xpk.at[pl.ds(part * part_rows, part_rows)]

    phases = {
        "w": (two, w_slot, w_own, wsend, wrecv),
        "x": (early, x_slot, x_own, xsend, xrecv),
        "a": (one, a_slot, None, asend, arecv),
    }

    def send_copies(phase, k, value):
        rounds, slot, own, send, recv = phases[phase]
        copies = []
        for from_z, link, chunk in rounds[k]:
            if from_z != value:
                continue
            src = slot(chunk)
            if own is not None and chunk[:3] == (0, 0, value):
                src = own(chunk[3])
            copies.append(remote(src, slot(chunk), send.at[k // 4, link], recv.at[k, link], links[link]))
        return copies

    def recv_copies(phase, k, value):
        rounds, slot, _, send, recv = phases[phase]
        copies = []
        for act in rounds[k]:
            to, chunk = landed(act)
            if to == value:
                copies.append(remote(slot(chunk), slot(chunk), send.at[k // 4, act[1]], recv.at[k, act[1]], links[act[1]]))
        return copies

    def start(phase, k, value):
        for copy in send_copies(phase, k, value):
            copy.start()

    def arrive(phase, k, value):
        for copy in recv_copies(phase, k, value):
            copy.wait_recv()

    back = (0, 1, 3, 2)

    def reduce_moves(k, value):
        out, come = [], []
        for act in one[last_one - k]:
            to, chunk = landed(act)
            if to == value:
                out.append((back[act[1]], chunk))
            if act[0] == value:
                come.append((back[act[1]], act[2]))
        return out, come

    def reduce_copies(k, value):
        return [
            remote(zacc.at[node_of(chunk)], rsb.at[k, link], rsend.at[link], rrecv.at[k, link], links[link])
            for link, chunk in reduce_moves(k, value)[0]
        ]

    def reduce_start(k, value):
        for copy in reduce_copies(k, value):
            copy.start()

    def reduce_arrive(k, value):
        for link, chunk in reduce_moves(k, value)[1]:
            remote(rsb.at[k, link], rsb.at[k, link], rsend.at[link], rrecv.at[k, link], links[link]).wait_recv()
            owner = node_of(chunk)
            zacc[owner] = zacc[owner] + rsb[k, link]

    copy_panels = pltpu.make_async_copy(g.at[:, pl.ds(0, pair)], gpa, local.at[0])
    own_pair = pl.ds(pl.multiple_of((me // 2) * pair, LANE), pair)
    copy_diag = pltpu.make_async_copy(g.at[:, own_pair], gt.at[0], local.at[1])
    copy_w = pltpu.make_async_copy(w, wv, local.at[2])
    copy_diag.start()
    copy_panels.start()
    copy_w.start()
    copy_diag.wait()
    on_diag = iota((rows, pair), 1) == iota((rows, pair), 0) + rows * (me % 2)
    trace = jnp.sum(jnp.where(on_diag, gt[0], 0.0), keepdims=True)
    trown[...] = jnp.broadcast_to(trace, trown.shape)
    trs[me] = jnp.broadcast_to(trace, trown.shape)
    trace_copies = [
        remote(trown, trs.at[me], tsem.at[0], tsem.at[1], (t, (me + k) % nodes)) for k in range(1, nodes)
    ]
    for copy in trace_copies:
        copy.start()
    by_z(lambda v: start("w", 0, v))
    copy_panels.wait()
    gpv[0] = gpa[:, 0:rows]
    gpv[1] = gpa[:, rows:pair]
    others = trs.at[pl.ds(0, nodes - 1)]
    remote(others, others, tsem.at[0], tsem.at[1], partner).wait_recv()
    total = jnp.sum(trs[...], axis=0)[0:1, 0:1]
    scale = width / total
    sv[...] = jnp.broadcast_to(scale, sv.shape)

    def panel(which):
        raw = gpv[which]
        eye = (iota((rows, rows), 0) == iota((rows, rows), 1)) & (me == which)
        return scale * (0.9 * raw + jnp.where(eye, 0.1 * raw, 0.0))

    xs[...] = panel(1 - t)
    swap = remote(xs, xrv, dsend.at[0], drecv.at[0], partner)
    swap.start()
    xrp[t] = jnp.zeros(xrp.shape[1:], f32)
    swap.wait_recv()
    xrp[t, :, 0:rows] = panel(t) + xrv[...]
    share = remote(xrp.at[t], xrp.at[t], dsend.at[1], drecv.at[1], partner)
    share.start()
    for h in range(2):
        for j in range(3):
            xpk[(3 * h + j) * half : (3 * h + j + 1) * half, :] = xrp[t, h * half : (h + 1) * half, j * LANE : (j + 1) * LANE]
    xpk[6 * half : 7 * half, :] = xrp[t, 0:half, 3 * LANE : PAD] + pltpu.roll(
        xrp[t, half:rows, 3 * LANE : PAD], LANE // 2, 1
    )
    own_x = pl.ds(pl.multiple_of(me * packed, 8), packed)
    store_x = pltpu.make_async_copy(xpk, xg.at[own_x], local.at[3])
    store_x.start()
    copy_w.wait()
    own_rows = pl.ds(pl.multiple_of(me * rows, rows), rows)
    store_w = pltpu.make_async_copy(wv, wg.at[own_rows], local.at[4])
    store_w.start()
    by_z(lambda v: start("x", 0, v))

    def products(which, into):
        high, low = halves(panel(which))
        xh[0:rows, 0:rows] = high
        xl[0:rows, 0:rows] = low

        @pl.loop(0, columns // PAD)
        def _(c):
            part = wv[:, pl.ds(pl.multiple_of(c * PAD, PAD), PAD)]
            value = bf(xh[0:rows, 0:rows], part, TN) + bf(xl[0:rows, 0:rows], part, TN)
            for q in range(PAD // LANE):
                into[c * (PAD // LANE) + q] = value[:, q * LANE : (q + 1) * LANE]

    products(1 - t, zsend)
    trade = remote(zsend, zrecv, dsend.at[2], drecv.at[2], partner)
    trade.start()
    by_z(lambda v: (arrive("x", 0, v), start("x", 1, v)))
    products(t, zacc)
    trade.wait()

    @pl.loop(0, blocks)
    def _(i):
        zacc[i] = zacc[i] + zrecv[i]

    def own_top(v):
        reduce_arrive(last_one, v)
        rt[me] = zacc[me]
        start("a", 0, v)

    by_z(lambda v: (arrive("x", 1, v), start("x", 2, v), reduce_start(0, v)))
    size = cw.shape[0]
    same = iota((size, size), 0) == iota((size, size), 1)
    li[...] = jnp.where(same, 1.0, 0.0)
    cw[...] = jnp.where(same & (iota((size, size), 0) % PAD >= rows), 1.0, 0.0)
    share.wait()
    store_x.wait()
    store_w.wait()
    for k in range(3, 6):
        by_z(
            lambda v, k=k: (
                arrive("x", k - 1, v), start("x", k, v), reduce_arrive(k - 3, v), reduce_start(k - 2, v)
            )
        )

    by_z(lambda v: (arrive("x", 5, v), start("x", 6, v)))
    fetch = pltpu.make_async_copy(xg.at[pl.ds(0, 2 * packed)], xpm, local.at[5])
    fetch.start()
    fetch.wait()
    give = remote(xpm, xpo, dsend.at[3], drecv.at[3], partner)
    give.start()

    low_lanes = iota((half, LANE), 1) < LANE // 2

    def tile(ref, h, j):
        if j < 3:
            return ref[(3 * h + j) * half : (3 * h + j + 1) * half, :]
        last = ref[6 * half : 7 * half, :]
        if h == 1:
            last = pltpu.roll(last, LANE // 2, 1)
        return jnp.where(low_lanes, last, 0.0)

    def place(ref, which):
        for k in range(2):
            for h in range(2):
                for j in range(4):
                    at = pl.ds(pl.multiple_of(which * PAD + j * LANE, LANE), LANE)
                    cw[k * PAD + h * half : k * PAD + (h + 1) * half, at] = tile(ref.at[k * packed : (k + 1) * packed], h, j)

    place(xpm, t)
    give.wait()
    place(xpo, 1 - t)

    def eliminate(k):
        o = pl.multiple_of(k * LANE, LANE)
        step, wide = 16, 2 * LANE
        own = pl.ds(o, LANE)
        groups = LANE // step - (LANE // step // 2) * ((k % 4) // 3)
        sub, lane, sub1 = iota((LANE, LANE), 0), iota((LANE, LANE), 1), iota((LANE, 1), 0)
        sub8, lane8 = iota((step, LANE), 0), iota((step, LANE), 1)
        dref[...] = cw[own, own]
        bref[...] = jnp.where(sub == lane, 1.0, 0.0)

        def pivots(i, carry):
            at = pl.multiple_of(i * step, step)
            here = pl.ds(at, step)
            rows8 = dref[here, :]
            for s in range(step):
                column = jnp.sum(jnp.where(lane8 == at + s, rows8, 0.0), axis=1, keepdims=True)
                cref[s, 0:step, :] = jnp.broadcast_to(column, (step, LANE))
            scaled = []
            for s in range(step):
                inverse = 1.0 / cref[s, s : s + 1, :]
                factor = jnp.where(sub8 > s, cref[s, 0:step, :] * inverse, 0.0)
                for later in range(s + 1, step):
                    cref[later, 0:step, :] = cref[later, 0:step, :] - factor * cref[later, s : s + 1, :]
                row, brow = dref[pl.ds(at + s, 1), :], bref[pl.ds(at + s, 1), :]
                dref[here, :] = dref[here, :] - factor * row
                bref[here, :] = bref[here, :] - factor * brow
                scaled.append(row * inverse)
            factors = jnp.transpose(jnp.concatenate(scaled * (LANE // step), axis=0))
            d, b = dref[...], bref[...]
            for s in range(step):
                factor = jnp.where(sub1 >= at + step, factors[:, s : s + 1], 0.0)
                d = d - factor * dref[pl.ds(at + s, 1), :]
                b = b - factor * bref[pl.ds(at + s, 1), :]
            dref[...] = d
            bref[...] = b
            return carry

        lax.fori_loop(0, groups, pivots, 0)
        diagonal = jnp.sum(jnp.where(sub == lane, dref[...], 0.0), axis=1, keepdims=True)
        bref[...] = bref[...] * lax.rsqrt(diagonal)
        first = (o + LANE) // wide
        last = (o + LANE + wide - 1) // wide
        count = size // wide

        def finish(n, carry):
            at = pl.ds(pl.multiple_of(n * wide, wide), wide)
            li[own, at] = mm(bref[...], li[own, at])
            return carry

        def ahead(n, carry):
            at = pl.ds(pl.multiple_of(n * wide, wide), wide)
            uref[:, at] = mm(bref[...], cw[own, at])
            return carry

        lax.fori_loop(0, last, finish, 0)
        lax.fori_loop(first, count, ahead, 0)

        def below(i, carry):
            at = pl.ds(pl.multiple_of(i * LANE, LANE), LANE)
            dref[...] = jnp.transpose(uref[:, at])

            def right(n, carry):
                to = pl.ds(pl.multiple_of(n * wide, wide), wide)
                cw[at, to] = cw[at, to] - mm(dref[...], uref[:, to])
                return carry

            def left(n, carry):
                to = pl.ds(pl.multiple_of(n * wide, wide), wide)
                li[at, to] = li[at, to] - mm(dref[...], li[own, to])
                return carry

            lax.fori_loop(first, count, right, 0)
            lax.fori_loop(0, last, left, 0)
            return carry

        lax.fori_loop(k + 1, size // LANE, below, 0)

    def coefficients():
        wide = 2 * LANE

        @pl.loop(0, size // wide)
        def _(c):
            at = pl.ds(pl.multiple_of(c * wide, wide), wide)
            cw[0:rows, at] = mm(xrp[0], li[at, 0:PAD], NT) + mm(xrp[1], li[at, PAD:size], NT)

        top = pl.ds(pl.multiple_of(jnp.minimum(me, 1) * PAD, PAD), rows)

        @pl.loop(0, PAD // wide)
        def _(c):
            at = pl.ds(pl.multiple_of(t * PAD + c * wide, wide), wide)
            to = pl.ds(pl.multiple_of(c * wide, wide), wide)
            lower = -mm(cw[0:rows, :], li[:, at])
            value = jnp.where(me < PANEL_STEPS, li[top, at], lower)
            ahl[0:rows, to], ahl[rows:pair, to] = halves(value)

    def own_block(ref, j):
        raw = ref[...]
        eye = iota((rows, pair), 1) + j * pair == iota((rows, pair), 0) + me * rows
        return sv[0:1, 0:1] * (0.9 * raw + jnp.where(eye, 0.1 * raw, 0.0))

    def gram_tile(j, slot, sem):
        return pltpu.make_async_copy(g.at[:, pl.ds(pl.multiple_of(j * pair, LANE), pair)], gt.at[slot], sem)

    def gram_pieces():
        def load(j, slot):
            return (
                gram_tile(j, slot, elocal.at[slot, 0]),
                pltpu.make_async_copy(
                    xg.at[pl.ds(pl.multiple_of(2 * j * packed, 8), 2 * packed)], xp2.at[slot], elocal.at[slot, 1]
                ),
            )

        def out(j, slot):
            tile_out = cw.at[pl.ds(pl.multiple_of(slot * PAD, PAD), rows), pl.ds(0, pair)]
            at = pl.ds(pl.multiple_of(j * pair, LANE), pair)
            return (
                pltpu.make_async_copy(tile_out, em.at[:, at], elocal.at[slot, 2]),
                remote(tile_out, eo.at[:, at], esend.at[j], erecv.at[j], partner),
            )

        for copy in load(0, 0):
            copy.start()

        def piece(j, carry):
            slot = j % 2
            for copy in load(j, slot):
                copy.wait()

            @pl.when(j + 1 < blocks // 2)
            def _():
                for copy in load(j + 1, 1 - slot):
                    copy.start()

            @pl.when(j >= 2)
            def _():
                keep, away = out(j - 2, slot)
                keep.wait()
                away.wait()

            for k in range(2):
                for h in range(2):
                    at = slice(k * rows + h * half, k * rows + (h + 1) * half)
                    for q in range(4):
                        high, low = halves(tile(xp2.at[slot, k * packed : (k + 1) * packed], h, q))
                        xh[at, q * LANE : (q + 1) * LANE] = high
                        xl[at, q * LANE : (q + 1) * LANE] = low
            both = bf(ahl[...], xh[...], NT)
            value = both[0:rows] + (both[rows:pair] + bf(ahl[0:rows, :], xl[...], NT))
            value = value + jnp.where(me >= PANEL_STEPS, own_block(gt.at[slot], j), 0.0)
            cw[pl.ds(pl.multiple_of(slot * PAD, PAD), rows), pl.ds(0, pair)] = value
            keep, away = out(j, slot)
            keep.start()
            away.start()
            return carry

        lax.fori_loop(0, blocks // 2, piece, 0)
        for j in (blocks // 2 - 2, blocks // 2 - 1):
            keep, away = out(j, j % 2)
            keep.wait()
            away.wait()

    orders, ready = pair_order(two)

    def weight_piece(position, arrived=lambda: None):
        b = [orders[v][position][0] for v in range(LINE)]
        s = [orders[v][position][1] for v in range(LINE)]

        def pick(values):
            chosen = values[LINE - 1]
            for v in range(LINE - 2, -1, -1):
                chosen = jnp.where(z == v, values[v], chosen)
            return chosen

        bb = pick(b)
        j = pick(s) * 2 + (y + bb - 2 * bb * y)
        load = gram_tile(j, position % 2, local.at[6])
        load.start()
        load.wait()
        high, low = halves(jnp.where(me >= PANEL_STEPS, own_block(gt.at[position % 2], j), 0.0))
        rhl[0:rows, :] = high
        rhl[rows:pair, :] = low
        arrived()
        rows_of = pl.ds(pl.multiple_of(j * pair, pair), pair)

        def part_copy(c):
            at = pl.ds(pl.multiple_of(c * PAD, PAD), PAD)
            return pltpu.make_async_copy(wg.at[rows_of, at], wt.at[c], wsem.at[c])

        for c in range(columns // PAD):
            part_copy(c).start()

        @pl.loop(0, columns // PAD)
        def _(c):
            part_copy(c).wait()
            both = bf(rhl[...], wt[c])
            value = both[0:rows] + both[rows:pair]
            for q in range(PAD // LANE):
                at = c * (PAD // LANE) + q
                piece = value[:, q * LANE : (q + 1) * LANE]
                zsend[at] = piece if position == 0 else zsend[at] + piece
            if position == SIDE * LINE - 1:
                for copy in rhs_out(c):
                    copy.start()

    def rhs_out(c):
        at = pl.ds(pl.multiple_of(c * (PAD // LANE), PAD // LANE), PAD // LANE)
        return (
            pltpu.make_async_copy(zsend.at[at], fm.at[at], flocal.at[c]),
            remote(zsend.at[at], fo.at[at], fsend.at[c], frecv.at[c], partner),
        )

    def top_share():
        @pl.loop(0, blocks)
        def _(i):
            high, low = halves(rt[i])
            both = bf(ahl[:, 0:rows], high)
            zsend[i] = zsend[i] + (both[0:rows] + (both[rows:pair] + bf(ahl[0:rows, 0:rows], low)))

    by_z(lambda v: (reduce_arrive(3, v), reduce_start(4, v), start("w", 1, v)))
    eliminate(0)
    by_z(lambda v: (arrive("x", 6, v), start("x", 7, v), own_top(v)))
    eliminate(1)
    by_z(lambda v: (arrive("x", 7, v), start("x", 8, v), arrive("a", 0, v), start("a", 1, v)))
    eliminate(2)
    by_z(lambda v: (arrive("x", 8, v), start("x", 9, v), arrive("a", 1, v), start("a", 2, v)))
    by_z(lambda v: (arrive("w", 0, v), start("w", 2, v)))
    lax.fori_loop(3, 5, lambda k, c: (eliminate(k), c)[1], 0)
    by_z(lambda v: (arrive("x", 9, v), arrive("a", 2, v), start("a", 3, v), arrive("w", 1, v), start("w", 3, v)))
    eliminate(5)
    by_z(lambda v: (arrive("a", 3, v), start("a", 4, v), arrive("w", 2, v), start("w", 4, v)))
    lax.fori_loop(6, 8, lambda k, c: (eliminate(k), c)[1], 0)
    by_z(lambda v: (arrive("w", 3, v), start("w", 5, v)))
    coefficients()
    gram_pieces()
    by_z(lambda v: (arrive("a", 4, v), arrive("w", 4, v), start("w", 6, v)))
    weight_piece(0)
    weight_piece(1)
    by_z(lambda v: (arrive("w", 5, v), start("w", 7, v)))
    weight_piece(2)
    top_share()
    by_z(lambda v: (arrive("w", 6, v), start("w", 8, v)))
    by_z(lambda v: (arrive("w", 7, v), start("w", 9, v)))
    weight_piece(3)
    weight_piece(4)
    weight_piece(5, lambda: by_z(lambda v: arrive("w", 8, v)))
    weight_piece(6)
    weight_piece(7, lambda: by_z(lambda v: arrive("w", 9, v)))
    for c in range(columns // PAD):
        for copy in rhs_out(c):
            copy.wait()

    for copy in trace_copies[:1]:
        remote(others, others, tsem.at[0], tsem.at[1], partner).wait_send()
    swap.wait_send()

    def drained(v):
        for link in range(4):
            for name, rounds, whole, rows_each in (("w", two, wg, half), ("x", early, xg, part_rows), ("a", one, rt, 1)):
                for first in range(0, len(rounds), 4):
                    count = sum(act[0] == v and act[1] == link for acts in rounds[first : first + 4] for act in acts)
                    sem = phases[name][3].at[first // 4, link]
                    if count:
                        all_of = whole.at[pl.ds(0, count * rows_each)]
                        remote(all_of, all_of, sem, sem, partner).wait_send()
            count = sum(move[0] == link for k in range(len(one)) for move in reduce_moves(k, v)[0])
            if count:
                all_of = zacc.at[pl.ds(0, count)]
                remote(all_of, all_of, rsend.at[link], rsend.at[link], partner).wait_send()

    by_z(drained)


def fused(parts, activation_grams, adjusted_weights):
    f32, b16 = jnp.float32, jnp.bfloat16
    gram, weights = activation_grams[0], adjusted_weights[0]
    rows, width = gram.shape
    columns = weights.shape[1]
    half, blocks, size = rows // 2, columns // LANE, PANEL_STEPS * PAD
    packed = 7 * half
    hbm = pl.BlockSpec(memory_space=pl.ANY)
    vmem, dma = pltpu.VMEM, pltpu.SemaphoreType.DMA
    block = (blocks, rows, LANE)
    rounds, short = len(TWO), len(ONE)
    em, eo, fm, fo, _, _ = pl.pallas_call(
        kernel,
        out_shape=[
            jax.ShapeDtypeStruct((rows, width), f32),
            jax.ShapeDtypeStruct((rows, width), f32),
            jax.ShapeDtypeStruct(block, f32),
            jax.ShapeDtypeStruct(block, f32),
            jax.ShapeDtypeStruct((parts * rows, columns), b16),
            jax.ShapeDtypeStruct((parts * packed, LANE), f32),
        ],
        in_specs=[hbm] * 2,
        out_specs=[hbm] * 6,
        scratch_shapes=[
            vmem((rows, 2 * rows), f32), vmem((2, rows, rows), f32), vmem((2, rows, 2 * rows), f32), vmem((rows, columns), b16),
            vmem((8, LANE), f32), vmem((parts, 8, LANE), f32), vmem((8, LANE), f32),
            vmem((rows, rows), f32), vmem((rows, rows), f32), vmem((2, rows, PAD), f32), vmem((packed, LANE), f32),
            vmem(block, f32), vmem(block, f32), vmem(block, f32), vmem((short, 4, rows, LANE), f32), vmem(block, f32),
            vmem((size, size), f32), vmem((size, size), f32),
            vmem((2 * packed, LANE), f32), vmem((2 * packed, LANE), f32), vmem((2, 2 * packed, LANE), f32),
            vmem((LANE, LANE), f32), vmem((LANE, LANE), f32), vmem((16, 16, LANE), f32), vmem((LANE, size), f32),
            vmem((2 * rows, PAD), b16), vmem((2 * rows, PAD), b16), vmem((2 * rows, PAD), b16),
            vmem((2 * rows, 2 * rows), b16), vmem((columns // PAD, 2 * rows, PAD), b16),
            dma((3, 4)), dma((rounds, 4)), dma((3, 4)), dma((rounds, 4)),
            dma((4,)), dma((short, 4)), dma((2, 4)), dma((short, 4)),
            dma((9,)), dma((2,)), dma((4,)), dma((4,)), dma((8,)), dma((8,)), dma((2, 3)), dma((4,)), dma((4,)), dma((4,)), dma((4,)),
        ],
        compiler_params=pltpu.CompilerParams(has_side_effects=True, vmem_limit_bytes=67043328),
        name="merge",
    )(gram, weights)
    rhs = jnp.transpose(fm + fo, (1, 0, 2)).reshape(rows, columns)
    return em + eo, rhs


def product(left, right):
    return jnp.dot(left, right, precision=lax.Precision.HIGHEST)


def inverse_of(factor):
    identity = jnp.eye(factor.shape[0], dtype=factor.dtype)
    return jax.scipy.linalg.solve_triangular(factor, identity, lower=True)


def leading_block(columns_block, parts, rows, wide):
    position = lax.axis_index("row")
    holders = wide // rows
    if rows % parts == 0:
        pieces = lax.all_to_all(
            columns_block.reshape(parts, rows // parts, wide), "row", 0, 0, tiled=True
        )[:holders]
        gathered = lax.all_gather(pieces, "row", axis=1, tiled=True)
        return gathered.reshape(wide, wide)
    placed = jnp.zeros((wide, wide), columns_block.dtype)
    kept = jnp.where(position < holders, columns_block, 0)
    start = jnp.minimum(position, holders - 1) * rows
    return lax.psum(lax.dynamic_update_slice_in_dim(placed, kept, start, 0), "row")


def per_device(parts, activation_grams, adjusted_weights):
    gram = activation_grams[0]
    rows, width = gram.shape
    columns = adjusted_weights.shape[2]
    wide = PANEL_STEPS * rows
    position = lax.axis_index("row")
    task = lax.axis_index("task")
    start_col = position * rows
    weights = lax.all_gather(adjusted_weights[0], "row", axis=0, tiled=True)

    own_block = lax.dynamic_slice_in_dim(gram, start_col, rows, 1)
    diagonal_entries = jnp.diagonal(own_block)
    scaling = width / lax.psum(jnp.sum(diagonal_entries), "row")
    row_ids = lax.broadcasted_iota(jnp.int32, (rows, width), 0) + start_col
    col_ids = lax.broadcasted_iota(jnp.int32, (rows, width), 1)
    source = scaling * (0.9 * gram + jnp.where(row_ids == col_ids, 0.1 * gram, 0.0))

    panel_cols = lax.psum(source[:, :wide], "task")
    corner = leading_block(panel_cols, parts, rows, wide)
    first_inverse = inverse_of(jnp.linalg.cholesky(corner[:rows, :rows]))
    left = product(corner[rows:, :rows], first_inverse.T)
    second = jnp.linalg.cholesky(corner[rows:, rows:] - product(left, left.T))
    second_inverse = inverse_of(second)
    coupling = -product(second_inverse, product(left, first_inverse))
    solver = jnp.where(
        task == 0,
        jnp.concatenate([first_inverse, jnp.zeros_like(first_inverse)], axis=1),
        jnp.concatenate([coupling, second_inverse], axis=1),
    )
    mine = product(solver, panel_cols.T)
    upper = lax.all_gather(mine, "row", axis=1, tiled=True)

    high = lax.reduce_precision(source, 8, 7)
    low = (source - high).astype(jnp.bfloat16)
    folded = jnp.dot(
        high.astype(jnp.bfloat16), weights, preferred_element_type=jnp.float32
    ) + jnp.dot(low, weights, preferred_element_type=jnp.float32)

    pieces = lax.all_to_all(folded, "row", 1, 0, tiled=True)
    held, solver = lax.optimization_barrier((pieces[:wide], solver))
    top = lax.psum(held, "task")
    solved = lax.all_gather(product(solver, top), "row", axis=1, tiled=True)

    below = position >= PANEL_STEPS
    holds = position == task
    merged_part = jnp.where(
        below, source - product(mine.T, upper), jnp.where(holds, upper, 0.0)
    )
    rhs_part = jnp.where(
        below, folded - product(mine.T, solved), jnp.where(holds, solved, 0.0)
    )
    return lax.psum((merged_part, rhs_part), "task")


def solution(mesh):
    assert mesh.shape["task"] == PANEL_STEPS
    parts = mesh.shape["row"]
    placed = (P("task", "row", None), P("task", "row", None))

    def run(grams, weights):
        rows, columns = grams.shape[1], weights.shape[2]
        fits = parts == SIDE * SIDE * LINE and rows == 7 * LANE // 2 and columns == parts * LANE
        return (fused if fits else per_device)(parts, grams, weights)

    return jax.shard_map(
        run,
        mesh=mesh,
        in_specs=placed,
        out_specs=(P("row", None), P("row", None)),
        check_vma=False,
    )
```

profile of v0, /device:TPU:0, one launch (start us, length us, event | category | flops | bytes accessed | tf_op | source)
XLA Modules:
  0.0 380.7 jit_solution(12770324035370089652)
XLA Ops:
  0.6 362.8 %merge.1 = (f32[448,7168]{1,0:T(8,128)}, f32[448,7168]{1,0:T(8,128)}, f32[16,448,128]{2,1,0:T(8,128)}, f32[16,448,128]{2,1,0:T(8,128)}, bf16[7168,2048]{1,0:T(8,128)(2,1)}, /*index=5*/f32[25088,128]{1,0:T(8,128)}) custom-call(f32[448,7168]{1,0:T(8,128)} %bitcast.8, bf16[448,2048]{1,0:T(8,128)(2,1)} %bitcast.9), custom_call_target="tpu_custom_call" | custom-call | tf_op jit(solution)/shard_map/merge/pallas_call | solution.py:630
  363.4 0.0 copy-start
  363.5 0.0 copy-start.1
  363.5 14.4 %add.6 = f32[448,7168]{1,0:T(8,128)} add(f32[448,7168]{1,0:T(8,128)} %get-tuple-element.6, f32[448,7168]{1,0:T(8,128)} %get-tuple-element.7) | non-fusion elementwise | flops 3211264 | bytes 38535168 | tf_op jit(solution)/shard_map/add | solution.py:660
  377.9 0.0 copy-done
  377.9 0.0 copy-done.1
  377.9 2.4 copy_bitcast_fusion
Async XLA Ops:
  363.4 14.4 %copy-start = (f32[16,448,128]{2,1,0:T(8,128)S(1)}, f32[16,448,128]{2,1,0:T(8,128)}, u32[]{:S(2)}) copy-start(f32[16,448,128]{2,1,0:T(8,128)} %get-tuple-element.8) | copy-start | bytes 11010052
  363.5 14.4 %copy-start.1 = (f32[16,448,128]{2,1,0:T(8,128)S(1)}, f32[16,448,128]{2,1,0:T(8,128)}, u32[]{:S(2)}) copy-start(f32[16,448,128]{2,1,0:T(8,128)} %get-tuple-element.9) | copy-start | bytes 11010052
where the time goes:
time: 387 us; the launch traced here: 381 us
  Pallas kernels  363 us (94%)
  other arithmetic  16.8 us (4%)
    pallas_call x1, Pallas kernels, fused(): pl.pallas_call(kernel, out_shape=[jax.ShapeDtypeStruct((rows, width), f32...  363 us
    add x1, other arithmetic, fused(): return (em + eo, rhs)  14.4 us

commit v1 on v0

--- a/solution.py
+++ b/solution.py
@@ -295,6 +295,7 @@
     @pl.loop(0, blocks)
     def _(i):
         zacc[i] = zacc[i] + zrecv[i]
+        zsend[i] = jnp.zeros(zsend.shape[1:], f32)
 
     def own_top(v):
         reduce_arrive(last_one, v)
@@ -508,21 +509,20 @@
     orders, ready = pair_order(two)
 
     def weight_piece(position, arrived=lambda: None):
-        b = [orders[v][position][0] for v in range(LINE)]
-        s = [orders[v][position][1] for v in range(LINE)]
-
-        def pick(values):
-            chosen = values[LINE - 1]
-            for v in range(LINE - 2, -1, -1):
-                chosen = jnp.where(z == v, values[v], chosen)
+        def pick(which):
+            chosen = 0
+            for p in range(SIDE * LINE):
+                for v in range(LINE):
+                    chosen = jnp.where((z == v) & (position == p), orders[v][p][which], chosen)
             return chosen
 
-        bb = pick(b)
-        j = pick(s) * 2 + (y + bb - 2 * bb * y)
-        load = gram_tile(j, position % 2, local.at[6])
+        b = pick(0)
+        j = pick(1) * 2 + (y + b - 2 * b * y)
+        final = isinstance(position, int)
+        load = gram_tile(j, 0, local.at[6])
         load.start()
         load.wait()
-        high, low = halves(jnp.where(me >= PANEL_STEPS, own_block(gt.at[position % 2], j), 0.0))
+        high, low = halves(jnp.where(me >= PANEL_STEPS, own_block(gt.at[0], j), 0.0))
         rhl[0:rows, :] = high
         rhl[rows:pair, :] = low
         arrived()
@@ -543,10 +543,13 @@
             for q in range(PAD // LANE):
                 at = c * (PAD // LANE) + q
                 piece = value[:, q * LANE : (q + 1) * LANE]
-                zsend[at] = piece if position == 0 else zsend[at] + piece
-            if position == SIDE * LINE - 1:
+                zsend[at] = zsend[at] + piece
+            if final:
                 for copy in rhs_out(c):
                     copy.start()
+
+    def weight_pieces(first, last):
+        lax.fori_loop(first, last, lambda k, c: (weight_piece(k), c)[1], 0)
 
     def rhs_out(c):
         at = pl.ds(pl.multiple_of(c * (PAD // LANE), PAD // LANE), PAD // LANE)
@@ -579,17 +582,15 @@
     coefficients()
     gram_pieces()
     by_z(lambda v: (arrive("a", 4, v), arrive("w", 4, v), start("w", 6, v)))
-    weight_piece(0)
-    weight_piece(1)
+    weight_pieces(0, 2)
     by_z(lambda v: (arrive("w", 5, v), start("w", 7, v)))
-    weight_piece(2)
+    weight_pieces(2, 3)
     top_share()
     by_z(lambda v: (arrive("w", 6, v), start("w", 8, v)))
     by_z(lambda v: (arrive("w", 7, v), start("w", 9, v)))
-    weight_piece(3)
-    weight_piece(4)
-    weight_piece(5, lambda: by_z(lambda v: arrive("w", 8, v)))
-    weight_piece(6)
+    weight_pieces(3, 5)
+    by_z(lambda v: arrive("w", 8, v))
+    weight_pieces(5, 7)
     weight_piece(7, lambda: by_z(lambda v: arrive("w", 9, v)))
     for c in range(columns // PAD):
         for copy in rhs_out(c):

time: 387 us -> 382 us (0.987); the launches traced: 381 us -> 381 us
  no operation moved by 1% of the time
where the time goes in v1:
time: 382 us; the launch traced here: 381 us
  Pallas kernels  364 us (95%)
  other arithmetic  16.8 us (4%)
    pallas_call x1, Pallas kernels, fused(): pl.pallas_call(kernel, out_shape=[jax.ShapeDtypeStruct((rows, width), f32...  364 us
    add x1, other arithmetic, fused(): return (em + eo, rhs)  14.4 us

profile of v1, /device:TPU:0, one launch (start us, length us, event | category | flops | bytes accessed | tf_op | source)
XLA Modules:
  0.0 381.4 jit_solution(13768988734821852962)
XLA Ops:
  0.6 364.0 %merge.1 = (f32[448,7168]{1,0:T(8,128)}, f32[448,7168]{1,0:T(8,128)}, f32[16,448,128]{2,1,0:T(8,128)}, f32[16,448,128]{2,1,0:T(8,128)}, bf16[7168,2048]{1,0:T(8,128)(2,1)}, /*index=5*/f32[25088,128]{1,0:T(8,128)}) custom-call(f32[448,7168]{1,0:T(8,128)} %bitcast.8, bf16[448,2048]{1,0:T(8,128)(2,1)} %bitcast.9), custom_call_target="tpu_custom_call" | custom-call | tf_op jit(solution)/shard_map/merge/pallas_call | solution.py:631
  364.6 0.0 copy-start
  364.6 0.0 copy-start.1
  364.6 14.4 %add.6 = f32[448,7168]{1,0:T(8,128)} add(f32[448,7168]{1,0:T(8,128)} %get-tuple-element.6, f32[448,7168]{1,0:T(8,128)} %get-tuple-element.7) | non-fusion elementwise | flops 3211264 | bytes 38535168 | tf_op jit(solution)/shard_map/add | solution.py:661
  379.0 0.0 copy-done
  379.0 0.0 copy-done.1
  379.0 2.4 copy_bitcast_fusion
Async XLA Ops:
  364.6 14.4 %copy-start = (f32[16,448,128]{2,1,0:T(8,128)S(1)}, f32[16,448,128]{2,1,0:T(8,128)}, u32[]{:S(2)}) copy-start(f32[16,448,128]{2,1,0:T(8,128)} %get-tuple-element.8) | copy-start | bytes 11010052
  364.6 14.4 %copy-start.1 = (f32[16,448,128]{2,1,0:T(8,128)S(1)}, f32[16,448,128]{2,1,0:T(8,128)}, u32[]{:S(2)}) copy-start(f32[16,448,128]{2,1,0:T(8,128)} %get-tuple-element.9) | copy-start | bytes 11010052
